TPU v7x, 8 devices: a whole 2x2x1 slice. The times are simulated.
8 devices in a mesh: dp: 1 (over z), kv: 2 (over y), dup: 4 (over x, core).
Axes of the slice: x: 2, y: 2, z: 1, core: 2. Of those that a mesh axis runs over, the one named last changes fastest.
Arguments:
- query: bfloat16 [256, 32, 128], P('dp', ('kv', 'dup'))
- k_cache: bfloat16 [256, 2, 4096, 128], P('dp', 'kv')
- v_cache: bfloat16 [256, 2, 4096, 128], P('dp', 'kv')
- lengths: int32 [256], P('dp')
- w_out: bfloat16 [4096, 4096], P(('kv', 'dup'))
Outputs:
- output: bfloat16 [256, 4096], P('dp', ('kv', 'dup'))
All inputs are finite; a program needn't handle non-finite values.
Results may differ from a plain program's by a relative error of at most 0.00871299.
Values are sent between devices in bfloat16 or wider.
A program may use at most 2.25 GiB of HBM per device.

v0:
```python
import jax
import jax.numpy as jnp
from jax import lax
from jax.sharding import PartitionSpec as P, NamedSharding


def solution(mesh):
    dup_size = mesh.shape['dup']

    def per_device(q_loc, k_loc, v_loc, len_loc, w_loc):
        row_count, own_heads, head_dim = q_loc.shape
        seq_len = k_loc.shape[2]
        key_span = seq_len // dup_size
        span_start = lax.axis_index('dup') * key_span
        q_group = lax.all_gather(q_loc, 'dup', axis=1, tiled=True)
        k_span = lax.dynamic_slice_in_dim(k_loc, span_start, key_span, axis=2).reshape(row_count, key_span, head_dim)
        v_span = lax.dynamic_slice_in_dim(v_loc, span_start, key_span, axis=2).reshape(row_count, key_span, head_dim)
        scores = jnp.einsum('bgd,bsd->bgs', q_group, k_span, preferred_element_type=jnp.float32) * (head_dim ** -0.5)
        positions = span_start + jnp.arange(key_span)
        key_valid = positions[None, None, :] < len_loc[:, None, None]
        scores = jnp.where(key_valid, scores, -1e30)
        peak_score = jnp.max(scores, axis=-1)
        weights = jnp.exp(scores - peak_score[..., None])
        prob_sum = jnp.sum(weights, axis=-1)
        weighted = jnp.einsum('bgs,bsd->bgd', weights.astype(jnp.bfloat16), v_span, preferred_element_type=jnp.float32)
        partial = (weighted / prob_sum[..., None]).astype(jnp.bfloat16).reshape(row_count, dup_size, own_heads, head_dim)
        part_stats = jnp.stack([peak_score, prob_sum], axis=-1).reshape(row_count, dup_size, own_heads, 2)
        partial = lax.all_to_all(partial, 'dup', split_axis=1, concat_axis=1, tiled=True)
        part_stats = lax.all_to_all(part_stats, 'dup', split_axis=1, concat_axis=1, tiled=True)
        part_peaks = part_stats[..., 0]
        part_sums = part_stats[..., 1]
        best_peak = jnp.max(part_peaks, axis=1, keepdims=True)
        part_mass = jnp.exp(part_peaks - best_peak) * part_sums
        part_coef = part_mass / jnp.sum(part_mass, axis=1, keepdims=True)
        merged = jnp.sum(part_coef[..., None] * partial.astype(jnp.float32), axis=1)
        attn_flat = merged.astype(jnp.bfloat16).reshape(row_count, own_heads * head_dim)
        proj_part = jnp.dot(attn_flat, w_loc, preferred_element_type=jnp.float32)
        y_shard = lax.psum_scatter(proj_part, ('kv', 'dup'), scatter_dimension=1, tiled=True)
        return y_shard.astype(jnp.bfloat16)

    return jax.shard_map(
        per_device,
        mesh=mesh,
        in_specs=(P('dp', ('kv', 'dup'), None), P('dp', 'kv', None, None), P('dp', 'kv', None, None), P('dp'), P(('kv', 'dup'), None)),
        out_specs=P('dp', ('kv', 'dup')),
        check_vma=False,
    )
```

profile of v0, /device:TPU:0, one launch (start us, length us, event | category | flops | bytes accessed | tf_op | source)
XLA Modules:
  0.0 174.8 jit_solution(5192567437483717360)
XLA Ops:
  6.5 0.0 all-gather.2.cloned.1.call-start
  6.5 1.7 copy.9
  8.2 0.0 all-gather.2.cloned.1.call-update
  8.3 0.9 broadcast_compare_fusion
  9.2 16.3 %all-gather.2.cloned.1.call-done = bf16[256,16,128]{2,0,1:T(8,128)(2,1)} async-done(((bf16[256,4,128]{2,0,1:T(8,128)(2,1)}), bf16[256,16,128]{2,0,1:T(8,128)(2,1)}) %all-gather.2.cloned.1.call-update) | async-done | bytes 1048592 | tf_op jit(solution)/shard_map/all_gather | solution.py:15
  25.4 31.2 %bitcast_reduce_fusion = (f32[256,16]{1,0:T(8,128)S(1)}, f32[256,1024,16]{1,2,0:T(8,128)}) fusion(pred[256,1024]{1,0:T(8,128)(4,1)S(1)} %broadcast_compare_fusion, bf16[256,16,128]{2,0,1:T(8,128)(2,1)} %all-gather.2.cloned.1.call-done, bf16[256,1,4096,128]{3,2,1,0:T(8,128)(2,1)} %param.6, s32[]{:T(128)S(6)} %select_n.11), kind=kOutput, calls=%fused_computation.7 | convolution fusion | flops 1086320640 | bytes 85213184 | tf_op jit(solution)/shard_map/bgd,bsd->bgs/dot_general | solution.py:18
  56.7 0.1 copy.11
  56.7 8.3 %fusion.8 = f32[256,16]{1,0:T(8,128)S(1)} fusion(f32[256,1024,16]{1,2,0:T(8,128)} %get-tuple-element.6, f32[256,16]{1,0:T(8,128)S(1)} %get-tuple-element.5, pred[256,1024]{1,0:T(8,128)(4,1)S(1)} %broadcast_compare_fusion), kind=kLoop, calls=%fused_computation.11 | loop fusion | flops 16773120 | bytes 17072128 | tf_op jit(solution)/shard_map/reduce_sum | solution.py:24
  65.1 0.1 copy.12
  65.2 0.6 copy.13
  65.8 3.3 %all-to-all-start = ((f32[256,4,4,2]{0,2,3,1:T(4,128)}), f32[256,4,4,2]{0,2,3,1:T(4,128)S(1)}, u32[]{:S(2)}, u32[]{:S(2)}) async-start(f32[256,4,4,2]{0,2,3,1:T(4,128)} %copy.13), calls=%async_computation | async-start | bytes 65536 | tf_op jit(solution)/shard_map/all_to_all | solution.py:29
  69.1 28.4 %divide_convert_fusion = bf16[256,16,128]{2,1,0:T(8,128)(2,1)S(1)} fusion(f32[256,16]{1,0:T(8,128)S(1)} %fusion.8, bf16[256,1,4096,128]{3,2,1,0:T(8,128)(2,1)} %param.7, s32[]{:T(128)S(6)} %select_n.11, f32[256,1024,16]{1,2,0:T(8,128)} %get-tuple-element.6, f32[256,16]{1,0:T(8,128)S(1)} %get-tuple-element.5, pred[256,1024]{1,0:T(8,128)(4,1)S(1)} %broadcast_compare_fusion), kind=kOutput, calls=%fused_computation.17 | convolution fusion | flops 1091567616 | bytes 85229568 | tf_op jit(solution)/shard_map/bgs,bsd->bgd/dot_general | solution.py:25
  97.5 1.4 copy.17
  98.8 0.0 all-to-all-done
  98.8 3.5 %all-to-all-start.1 = ((bf16[256,4,4,128]{3,2,0,1:T(4,128)(2,1)}), bf16[256,4,4,128]{3,2,0,1:T(4,128)(2,1)S(1)}, u32[]{:S(2)}, u32[]{:S(2)}) async-start(bf16[256,4,4,128]{3,2,0,1:T(4,128)(2,1)} %copy.17), calls=%async_computation.1 | async-start | bytes 2097152 | tf_op jit(solution)/shard_map/all_to_all | solution.py:28
  102.4 0.0 reduce-scatter.2.cloned.1.call-start
  102.5 0.2 copy.16
  102.7 13.8 %all-to-all-done.1 = bf16[256,4,4,128]{3,2,0,1:T(4,128)(2,1)S(1)} async-done(((bf16[256,4,4,128]{3,2,0,1:T(4,128)(2,1)}), bf16[256,4,4,128]{3,2,0,1:T(4,128)(2,1)S(1)}, u32[]{:S(2)}, u32[]{:S(2)}) %all-to-all-start.1) | async-done | bytes 1048608 | tf_op jit(solution)/shard_map/all_to_all | solution.py:28
  116.5 1.7 multiply_reduce_fusion
  118.2 5.4 %fusion.19 = f32[256,4096]{1,0:T(8,128)} fusion(bf16[512,4096]{1,0:T(8,128)(2,1)} %param.9, bf16[32,8,4,128]{3,2,1,0:T(4,128)(2,1)S(1)} %bitcast.61), kind=kOutput, calls=%fused_computation.20 | convolution fusion | flops 1073741824 | bytes 8650752 | tf_op jit(solution)/shard_map/dot_general | solution.py:37
  123.6 0.0 reduce-scatter.2.cloned.1.call-update
  123.6 42.6 %reduce-scatter.2.cloned.1.call-done = f32[256,512]{1,0:T(8,128)} async-done(((f32[256,4096]{1,0:T(8,128)}), f32[256,512]{1,0:T(8,128)}) %reduce-scatter.2.cloned.1.call-update) | async-done | bytes 524304 | tf_op jit(solution)/shard_map/reduce_scatter | solution.py:38
  166.2 1.8 %convert_element_type.24 = bf16[256,512]{1,0:T(8,128)(2,1)} convert(f32[256,512]{1,0:T(8,128)} %reduce-scatter.2.cloned.1.call-done) | non-fusion elementwise | flops 131072 | bytes 786432 | tf_op jit(solution)/shard_map/convert_element_type | solution.py:39
  (7 shorter events, 0.1 us)
Async XLA Ops:
  6.5 18.9 %all-gather.2.cloned.1.call-start = ((), (), s32[]{:S(2)}) async-start(), calls=%async_computation.3 | async-start | bytes 1310720 | tf_op jit(solution)/shard_map/all_gather | solution.py:15
  65.8 33.0 %all-to-all-start = ((f32[256,4,4,2]{0,2,3,1:T(4,128)}), f32[256,4,4,2]{0,2,3,1:T(4,128)S(1)}, u32[]{:S(2)}, u32[]{:S(2)}) async-start(f32[256,4,4,2]{0,2,3,1:T(4,128)} %copy.13), calls=%async_computation | async-start | bytes 65536 | tf_op jit(solution)/shard_map/all_to_all | solution.py:29
  98.8 17.7 %all-to-all-start.1 = ((bf16[256,4,4,128]{3,2,0,1:T(4,128)(2,1)}), bf16[256,4,4,128]{3,2,0,1:T(4,128)(2,1)S(1)}, u32[]{:S(2)}, u32[]{:S(2)}) async-start(bf16[256,4,4,128]{3,2,0,1:T(4,128)(2,1)} %copy.17), calls=%async_computation.1 | async-start | bytes 2097152 | tf_op jit(solution)/shard_map/all_to_all | solution.py:28
  102.4 63.9 %reduce-scatter.2.cloned.1.call-start = ((), (), s32[]{:S(2)}) async-start(), calls=%async_computation.4 | async-start | bytes 4718592 | tf_op jit(solution)/shard_map/reduce_scatter | solution.py:38
Sparse Core Ops, SparseCore 0:
  8.9 16.5 all-gather.1
  123.8 42.4 reduce-scatter.1
where the time goes:
time: 175 us
  waiting for transfers between devices  72.7 us (42%)
  matrix products  65 us (37%)
  between operations  13.5 us (8%)
  other arithmetic  12.7 us (7%)
  starting transfers between devices  6.82 us (4%)
  local copies, waits for them, and re-layouts  4.02 us (2%)
    reduce_scatter x1, waiting for transfers between devices, per_device(): lax.psum_scatter(proj_part, ('kv', 'dup'), scatter_dimension=1, tiled=True)  42.6 us
    dot_general x1, matrix products, per_device(): jnp.einsum('bgd,bsd->bgs', q_group, k_span, preferred_element_type=jnp.fl...  31.2 us
    dot_general x1, matrix products, per_device(): jnp.einsum('bgs,bsd->bgd', weights.astype(jnp.bfloat16), v_span, preferre...  28.4 us
    all_gather x1, waiting for transfers between devices, per_device(): q_group = lax.all_gather(q_loc, 'dup', axis=1, tiled=True)  16.3 us
    all_to_all x1, waiting for transfers between devices, per_device(): lax.all_to_all(partial, 'dup', split_axis=1, concat_axis=1, tiled=True)  13.8 us
    reduce_sum x1, other arithmetic, per_device(): prob_sum = jnp.sum(weights, axis=-1)  8.31 us
    dot_general x1, matrix products, per_device(): proj_part = jnp.dot(attn_flat, w_loc, preferred_element_type=jnp.float32)  5.39 us
    all_to_all x1, starting transfers between devices, per_device(): lax.all_to_all(partial, 'dup', split_axis=1, concat_axis=1, tiled=True)  3.52 us
  transfers between devices with their start and end apart: 4, of which 3 were waited for; matrix products, arithmetic and copies ran while one was open for 18% of the time, Pallas kernels for 0%

commit v1 on v0

v1 whole, which is shorter than its diff:
```python
import functools
import math

import jax
import jax.numpy as jnp
from jax import lax
from jax.experimental import pallas as pl
from jax.experimental.pallas import tpu as pltpu
from jax.sharding import PartitionSpec as P

R = 64
T = 1024
H = 16
D = 128
C = (D ** -0.5) * math.log2(math.e)
NEG = -3.0e38
MESH = pl.DeviceIdType.MESH


def _peer(dup=None, kv=None):
    d = {}
    if dup is not None:
        d['dup'] = dup
    if kv is not None:
        d['kv'] = kv
    return d


def _rcopy(src, dst, ssem, rsem, dev):
    return pltpu.make_async_remote_copy(src_ref=src, dst_ref=dst, send_sem=ssem, recv_sem=rsem,
                                        device_id=dev, device_id_type=MESH)


def _enter(peers):
    barrier = pltpu.get_barrier_semaphore()
    for p in peers:
        pl.semaphore_signal(barrier, inc=1, device_id=p, device_id_type=MESH)
    pl.semaphore_wait(barrier, len(peers))


def spread_kernel(q_ref, w_ref, qr_ref, wp_ref, ssem, rsem, wssem, wrsem):
    me = lax.axis_index('dup')
    core = lax.rem(me, 2)
    mate = me + 1 - 2 * core
    _enter([_peer(dup=lax.rem(me + k, 4)) for k in (1, 2, 3)])
    cps = []
    for k in (2, 1, 3):
        to = lax.rem(me + k, 4)
        cps.append(_rcopy(q_ref.at[pl.ds(to * R, R)], qr_ref.at[me], ssem.at[k - 1], rsem.at[k - 1], _peer(dup=to)))
    for j in range(4):
        col = ((j // 2) * 4 + 2 * (j % 2) + (1 - core)) * 512
        cps.append(_rcopy(w_ref.at[:, pl.ds(pl.multiple_of(col, 512), 512)], wp_ref.at[:, pl.ds(j * 512, 512)],
                          wssem.at[j], wrsem.at[j], _peer(dup=mate)))
    for c in cps:
        c.start()
    for c in cps:
        c.wait()


def spread(q, w):
    any_ = pl.BlockSpec(memory_space=pl.ANY)
    dma = pltpu.SemaphoreType.DMA
    return pl.pallas_call(
        spread_kernel,
        out_shape=(jax.ShapeDtypeStruct((4, R, 4, D), jnp.bfloat16), jax.ShapeDtypeStruct((512, 2048), jnp.bfloat16)),
        in_specs=[any_, any_], out_specs=(any_, any_),
        scratch_shapes=[dma((3,)), dma((3,)), dma((4,)), dma((4,))],
        compiler_params=pltpu.CompilerParams(collective_id=0, has_side_effects=True),
        name='spread',
    )(q, w)


def attn_kernel(U, NBUF, len_ref, q_own, q_recv, k_ref, v_ref, o_ref,
                qv, q32, qt, kv, sbuf, o32, qsem, sem):
    me = lax.axis_index('dup')
    base = me * R

    def fetch(idx, row, tile, slot, n, start):
        length = len_ref[base + row]
        rem = length - tile * T
        pos = tile * T
        def go(off, size):
            if start:
                for j, src in enumerate((k_ref, v_ref)):
                    pltpu.make_async_copy(
                        src.at[base + row, 0, pl.ds(pos + off, size), :],
                        kv.at[slot, j, pl.ds(off, size), :], sem.at[slot]).start()
            else:
                part = kv.at[slot, :, pl.ds(off, size), :]
                pltpu.make_async_copy(part, part, sem.at[slot]).wait()
        full = jnp.logical_or(rem > 3 * T // 4, idx < NBUF)
        valid = idx < n
        @pl.when(jnp.logical_and(valid, full))
        def _():
            go(0, T)
        @pl.when(jnp.logical_and(valid, jnp.logical_not(full)))
        def _():
            lax.fori_loop(0, (rem + T // 4 - 1) // (T // 4), lambda i, c: (go(i * (T // 4), T // 4), c)[1], 0)

    def advance(row, tile):
        length = len_ref[base + jnp.minimum(row, R - 1)]
        done = (tile + 1) * T >= length
        return jnp.where(done, jnp.minimum(row + 1, R - 1), row), jnp.where(done, 0, tile + 1)

    n = lax.fori_loop(0, R, lambda i, s: s + (len_ref[base + i] + T - 1) // T, jnp.int32(0))

    qcp = [pltpu.make_async_copy(q_recv.at[lax.rem(me + k, 4)], qv.at[lax.rem(me + k, 4)], qsem.at[k]) for k in range(1, 4)]
    qcp.append(pltpu.make_async_copy(q_own.at[pl.ds(base, R)], qv.at[me], qsem.at[0]))
    for c in qcp:
        c.start()

    def prime(i, st):
        row, tile = st
        fetch(i, row, tile, i, n, True)
        return advance(row, tile)
    prow, ptile = lax.fori_loop(0, NBUF, prime, (jnp.int32(0), jnp.int32(0)))

    for c in qcp:
        c.wait()
    for s in range(4):
        q32[:, 4 * s:4 * s + 4, :] = qv[s].astype(jnp.float32)

    def prep(r, _):
        q16 = q32[r].astype(jnp.bfloat16)
        z16 = jnp.zeros_like(q16)
        qt[r] = jnp.concatenate([jnp.concatenate([q16, z16], 1), jnp.concatenate([z16, q16], 1)], 0)
        return 0
    lax.fori_loop(0, R, prep, 0, unroll=4)

    HT = T // 2
    pos_i = (lax.broadcasted_iota(jnp.int32, (2 * H, HT), 0) // H) * HT + lax.broadcasted_iota(jnp.int32, (2 * H, HT), 1)

    def scores(slot, row):
        kab = jnp.concatenate([kv[slot, 0, 0:HT, :], kv[slot, 0, HT:T, :]], axis=1)
        return lax.dot_general(qt[row], kab, (((1,), (1,)), ((), ())), preferred_element_type=jnp.float32)

    def rest(jobs, ss):
        ss = [jnp.where(pos_i < rem, s, NEG) for s, (_, _, rem) in zip(ss, jobs)]
        ms = [jnp.max(jnp.maximum(s[0:H], s[H:]), axis=1, keepdims=True) for s in ss]
        ps = [jnp.exp2((s - jnp.concatenate([m, m], 0)) * C) for s, m in zip(ss, ms)]
        ls = [jnp.sum(p[0:H] + p[H:], axis=1, keepdims=True) for p in ps]
        pbs = [p.astype(jnp.bfloat16) for p in ps]
        accs = []
        for pb, (slot, _, _) in zip(pbs, jobs):
            vab = jnp.concatenate([kv[slot, 1, 0:HT, :], kv[slot, 1, HT:T, :]], axis=1)
            o2 = jnp.dot(pb, vab, preferred_element_type=jnp.float32)
            accs.append(o2[0:H, 0:D] + o2[H:, D:])
        return list(zip(ms, ls, accs))

    NG = NBUF // U
    def group(g, crow, ctile):
        infos = []
        for u in range(U):
            infos.append((g * U + u, lax.rem(g, NG) * U + u, crow, ctile))
            crow, ctile = advance(crow, ctile)
        return infos, crow, ctile

    def wait_group(infos):
        for idx, slot, row, tile in infos:
            fetch(idx, row, tile, slot, n, False)

    def body(g, carry):
        prow, ptile, crow, ctile, m0, l0, a0 = carry
        infos, nrow, ntile = group(g, crow, ctile)
        nxt, _, _ = group(g + 1, nrow, ntile)
        wait_group(nxt)
        jobs = [(slot, row, jnp.where(idx < n, len_ref[base + row] - tile * T, 0)) for idx, slot, row, tile in infos]
        cur, oth = lax.rem(g, 2), lax.rem(g + 1, 2)
        ss = [sbuf[cur, u] for u in range(U)]
        nss = [scores(slot, row) for _, slot, row, _ in nxt]
        outs = rest(jobs, ss)
        for (idx, slot, row, tile), (m, l, acc) in zip(infos, outs):
            mp = jnp.where(tile == 0, NEG, m0)
            mn = jnp.maximum(mp, m)
            a = jnp.exp2((mp - mn) * C)
            b = jnp.exp2((m - mn) * C)
            m0 = mn
            l0 = l0 * a + l * b
            a0 = a0 * a + acc * b
            orow = jnp.where(idx < n, row, R)
            o32[orow] = a0 / l0
        for u in range(U):
            sbuf[oth, u] = nss[u]
        for idx, slot, row, tile in infos:
            fetch(idx + NBUF, prow, ptile, slot, n, True)
            prow, ptile = advance(prow, ptile)
        return prow, ptile, nrow, ntile, m0, l0, a0

    first, _, _ = group(jnp.int32(0), jnp.int32(0), jnp.int32(0))
    wait_group(first)
    for u, (_, slot, row, _) in enumerate(first):
        sbuf[0, u] = scores(slot, row)

    z = jnp.int32(0)
    init = (prow, ptile, z, z, jnp.full((H, 1), NEG, jnp.float32), jnp.ones((H, 1), jnp.float32), jnp.zeros((H, D), jnp.float32))
    lax.fori_loop(0, (n + U - 1) // U, body, init)
    for h in range(H):
        o_ref[h] = o32[0:R, h, :].astype(jnp.bfloat16)


def attention(q_own, q_recv, k, v, lens, U=4, NBUF=20):
    any_ = pl.BlockSpec(memory_space=pl.ANY)
    return pl.pallas_call(
        functools.partial(attn_kernel, U, NBUF),
        out_shape=jax.ShapeDtypeStruct((H, R, D), jnp.bfloat16),
        in_specs=[pl.BlockSpec(memory_space=pltpu.SMEM), any_, any_, any_, any_],
        out_specs=pl.BlockSpec(memory_space=pltpu.VMEM),
        scratch_shapes=[
            pltpu.VMEM((4, R, 4, D), jnp.bfloat16),
            pltpu.VMEM((R, H, D), jnp.float32),
            pltpu.VMEM((R, 2 * H, 2 * D), jnp.bfloat16),
            pltpu.VMEM((NBUF, 2, T, D), jnp.bfloat16),
            pltpu.VMEM((2, U, 2 * H, T // 2), jnp.float32),
            pltpu.VMEM((R + 1, H, D), jnp.float32),
            pltpu.SemaphoreType.DMA((4,)),
            pltpu.SemaphoreType.DMA((NBUF,)),
        ],
        compiler_params=pltpu.CompilerParams(vmem_limit_bytes=56 * 2**20),
        name='attn',
    )(lens, q_own, q_recv, k, v)

def proj_kernel(o_ref, w_ref, wp_ref, y_ref, oc, wv, pbuf, r1a, r1b, r2a, r2b,
                lsem, wsem, os, orr, s1s, s1a, s1b, s2s, s2a, s2b):
    me = lax.axis_index('dup')
    kv = lax.axis_index('kv')
    core = lax.rem(me, 2)
    x = me // 2
    ox, okv = 1 - x, 1 - kv
    mate = me + 1 - 2 * core
    far = lax.rem(me + 2, 4)
    mfar = lax.rem(mate + 2, 4)
    to_mate, to_x, to_y = _peer(dup=mate), _peer(dup=far), _peer(kv=okv)

    own = pltpu.make_async_copy(o_ref.at[pl.ds(x * 8, 8)], oc.at[me], lsem)
    own.start()
    wcps = []
    for i, (j, _) in enumerate(((okv * 2 + ox, 0), (kv * 2 + ox, 0), (okv * 2 + x, 0), (kv * 2 + x, 0))):
        col = pl.multiple_of((j * 2 + core) * 512, 512)
        wcps.append(pltpu.make_async_copy(w_ref.at[:, pl.ds(col, 512)], wv.at[j, pl.ds(core * 512, 512)], wsem.at[2 * i]))
        wcps.append(pltpu.make_async_copy(wp_ref.at[:, pl.ds(pl.multiple_of(j * 512, 512), 512)],
                                          wv.at[j, pl.ds((1 - core) * 512, 512)], wsem.at[2 * i + 1]))
    for c in wcps:
        c.start()
    _enter([to_mate, to_x, to_y])
    o_x = _rcopy(o_ref.at[pl.ds(ox * 8, 8)], oc.at[me], os.at[0], orr.at[0], to_x)
    o_x.start()
    o_m = _rcopy(o_ref.at[pl.ds(x * 8, 8)], oc.at[me], os.at[1], orr.at[1], to_mate)
    o_m.start()

    order = (okv * 2 + ox, kv * 2 + ox, okv * 2 + x, kv * 2 + x)
    fwd = None
    sends = []
    for t in range(2):
        X = x if t == 0 else ox
        if t == 0:
            own.wait()
            o_m.wait()
        else:
            fwd.wait()
        lhs = jnp.concatenate(
            [jnp.concatenate([oc[2 * X, h], oc[2 * X + 1, h]], axis=0) for h in range(8)], axis=1)
        for i, j in enumerate(order):
            if t == 0:
                wcps[2 * i].wait()
                wcps[2 * i + 1].wait()
            part = jnp.dot(lhs, wv[j], preferred_element_type=jnp.float32)
            pbuf[X, j, 0] = part[:, :256]
            pbuf[X, j, 1] = part[:, 256:]
            if i in (0, 1):
                k = okv if i == 0 else kv
                c = _rcopy(pbuf.at[X, j, 0], r1a.at[X, k], s1s.at[t, 2 * i], s1a.at[X, k], to_x)
                c.start()
                sends.append(c)
            if i in (0, 2):
                xx = ox if i == 0 else x
                c = _rcopy(pbuf.at[X, j, 1], r1b.at[X, xx], s1s.at[t, i + 1], s1b.at[X, xx], to_y)
                c.start()
                sends.append(c)
        if t == 0:
            o_x.wait()
            fwd = _rcopy(oc.at[far], oc.at[far], os.at[2], orr.at[2], to_mate)
            fwd.start()
    jm = kv * 2 + x
    for t in range(2):
        Xa = ox if t == 0 else x
        Xb = x if t == 0 else ox
        ja = okv * 2 + x
        _rcopy(pbuf.at[Xa, ja, 0], r1a.at[Xa, okv], s1s.at[0, 0], s1a.at[Xa, okv], to_x).wait_recv()
        pbuf[Xa, ja, 0] = pbuf[Xa, ja, 0] + r1a[Xa, okv]
        c = _rcopy(pbuf.at[Xa, ja, 0], r2a.at[Xa], s2s.at[t, 0], s2a.at[Xa], to_y)
        c.start()
        sends.append(c)
        jb = kv * 2 + ox
        _rcopy(pbuf.at[Xb, jb, 1], r1b.at[Xb, ox], s1s.at[0, 0], s1b.at[Xb, ox], to_y).wait_recv()
        pbuf[Xb, jb, 1] = pbuf[Xb, jb, 1] + r1b[Xb, ox]
        c = _rcopy(pbuf.at[Xb, jb, 1], r2b.at[Xb], s2s.at[t, 1], s2b.at[Xb], to_x)
        c.start()
        sends.append(c)
        _rcopy(pbuf.at[Xa, jm, 0], r1a.at[Xa, kv], s1s.at[0, 0], s1a.at[Xa, kv], to_x).wait_recv()
        pbuf[Xa, jm, 0] = pbuf[Xa, jm, 0] + r1a[Xa, kv]
        _rcopy(pbuf.at[Xb, jm, 1], r1b.at[Xb, x], s1s.at[0, 0], s1b.at[Xb, x], to_y).wait_recv()
        pbuf[Xb, jm, 1] = pbuf[Xb, jm, 1] + r1b[Xb, x]
    for t in range(2):
        Xa = ox if t == 0 else x
        Xb = x if t == 0 else ox
        _rcopy(pbuf.at[Xa, jm, 0], r2a.at[Xa], s1s.at[0, 0], s2a.at[Xa], to_y).wait_recv()
        y_ref[pl.ds(pl.multiple_of(Xa * 128, 128), 128), 0:256] = (pbuf[Xa, jm, 0] + r2a[Xa]).astype(jnp.bfloat16)
        Xb = ox if t == 0 else x
        _rcopy(pbuf.at[Xb, jm, 1], r2b.at[Xb], s1s.at[0, 0], s2b.at[Xb], to_x).wait_recv()
        y_ref[pl.ds(pl.multiple_of(Xb * 128, 128), 128), 256:512] = (pbuf[Xb, jm, 1] + r2b[Xb]).astype(jnp.bfloat16)
    for c in sends:
        c.wait_send()


def project(o, w, wp):
    any_ = pl.BlockSpec(memory_space=pl.ANY)
    dma = pltpu.SemaphoreType.DMA
    f32 = jnp.float32
    return pl.pallas_call(
        proj_kernel,
        out_shape=jax.ShapeDtypeStruct((256, 512), jnp.bfloat16),
        in_specs=[any_] * 3, out_specs=pl.BlockSpec(memory_space=pltpu.VMEM),
        scratch_shapes=[
            pltpu.VMEM((4, 8, R, D), jnp.bfloat16), pltpu.VMEM((4, 1024, 512), jnp.bfloat16),
            pltpu.VMEM((2, 4, 2, 128, 256), f32),
            pltpu.VMEM((2, 2, 128, 256), f32), pltpu.VMEM((2, 2, 128, 256), f32),
            pltpu.VMEM((2, 128, 256), f32), pltpu.VMEM((2, 128, 256), f32),
            dma, dma((8,)), dma((3,)), dma((3,)), dma((2, 4)), dma((2, 2)), dma((2, 2)),
            dma((2, 2)), dma((2,)), dma((2,)),
        ],
        compiler_params=pltpu.CompilerParams(collective_id=1, has_side_effects=True),
        name='project',
    )(o, w, wp)


def solution(mesh):
    def per_device(q, k, v, lens, w):
        q_recv, w_mate = spread(q, w)
        o = attention(q, q_recv, k, v, lens)
        return project(o, w, w_mate)

    return jax.shard_map(
        per_device,
        mesh=mesh,
        in_specs=(P('dp', ('kv', 'dup'), None), P('dp', 'kv', None, None), P('dp', 'kv', None, None), P('dp'), P(('kv', 'dup'), None)),
        out_specs=P('dp', ('kv', 'dup')),
        check_vma=False,
    )
```

time: 175 us -> 72.6 us (0.41)
  waiting for transfers between devices: 72.7 us -> 0 us
  Pallas kernels: 0 us -> 71 us
  matrix products: 65 us -> 0 us
  between operations: 13.5 us -> 0.02 us
  other arithmetic: 12.7 us -> 0 us
  starting transfers between devices: 6.82 us -> 0 us
  local copies, waits for them, and re-layouts: 4.02 us -> 1.67 us
    pallas_call x0 -> x3, Pallas kernels: none -> 71 us  [the longest x1 38.7 us: attention(): pl.pallas_call(functools.partial(attn_kernel, U, NBUF), out_shape=jax.Sha...]
    dot_general x3 -> x0, matrix products: 65 us -> none  [the longest x1 31.2 us: per_device(): jnp.einsum('bgd,bsd->bgs', q_group, k_span, preferred_element_type=jnp.fl...]
    reduce_scatter x1 -> x0, waiting for transfers between devices: 42.6 us -> none  [per_device(): lax.psum_scatter(proj_part, ('kv', 'dup'), scatter_dimension=1, tiled=True)]
    all_gather x1 -> x0, waiting for transfers between devices: 16.3 us -> none  [per_device(): q_group = lax.all_gather(q_loc, 'dup', axis=1, tiled=True)]
    all_to_all x2 -> x0, waiting for transfers between devices: 13.8 us -> none  [the longest x1 13.8 us: per_device(): lax.all_to_all(partial, 'dup', split_axis=1, concat_axis=1, tiled=True)]
    reduce_sum x3 -> x0, other arithmetic: 10 us -> none  [the longest x1 8.31 us: per_device(): prob_sum = jnp.sum(weights, axis=-1)]
    all_to_all x2 -> x0, starting transfers between devices: 6.78 us -> none  [the longest x1 3.52 us: per_device(): lax.all_to_all(partial, 'dup', split_axis=1, concat_axis=1, tiled=True)]
    convert_element_type x1 -> x0, other arithmetic: 1.77 us -> none  [per_device(): return y_shard.astype(jnp.bfloat16)]
  transfers between devices with their start and end apart: 4 -> 0, of which waited for: 3 -> 0; matrix products, arithmetic and copies ran while one was open for 18% -> 0% of each run, Pallas kernels for 0% -> 0%
where the time goes in v1:
time: 72.6 us; the launch traced here: 72.7 us
  Pallas kernels  71 us (98%)
  local copies, waits for them, and re-layouts  1.67 us (2%)
    pallas_call x1, Pallas kernels, attention(): pl.pallas_call(functools.partial(attn_kernel, U, NBUF), out_shape=jax.Sha...  38.7 us
    pallas_call x1, Pallas kernels, project(): pl.pallas_call(proj_kernel, out_shape=jax.ShapeDtypeStruct((256, 512), jn...  24.9 us
    pallas_call x1, Pallas kernels, spread(): pl.pallas_call(spread_kernel, out_shape=(jax.ShapeDtypeStruct((4, R, 4, D...  7.46 us
    unnamed x1, local copies, waits for them, and re-layouts  1.67 us

profile of v1, /device:TPU:0, one launch (start us, length us, event | category | flops | bytes accessed | tf_op | source)
XLA Modules:
  0.0 72.7 jit_solution(2483795859960780394)
XLA Ops:
  0.0 7.5 %spread.1 = (bf16[4,64,4,128]{3,2,1,0:T(4,128)(2,1)}, bf16[512,2048]{1,0:T(8,128)(2,1)}) custom-call(bf16[256,4,128]{2,1,0:T(4,128)(2,1)} %q_own.1, bf16[512,4096]{1,0:T(8,128)(2,1)} %w_ref.3), custom_call_target="tpu_custom_call" | custom-call | tf_op jit(solution)/shard_map/spread/pallas_call | solution.py:63
  7.5 38.7 %attn.1.o_ref = bf16[16,64,128]{2,1,0:T(8,128)(2,1)} custom-call(s32[256]{0:T(256)} %len_ref.1, bf16[256,4,128]{2,1,0:T(4,128)(2,1)} %q_own.1, bf16[4,64,4,128]{3,2,1,0:T(4,128)(2,1)} %get-tuple-element.7.q_recv, bf16[256,1,4096,128]{3,2,1,0:T(8,128)(2,1)} %k_ref.1, bf16[256,1,4096,128]{3,2,1,0:T(8,128)(2,1)} %v_ref.1), custom_call_target="tpu_custom_call" | custom-call | tf_op jit(solution)/shard_map/attn/pallas_call | solution.py:203
  46.1 24.9 %project.1 = bf16[256,512]{1,0:T(8,128)(2,1)} custom-call(bf16[16,64,128]{2,1,0:T(8,128)(2,1)} %attn.1.o_ref, bf16[512,4096]{1,0:T(8,128)(2,1)} %w_ref.3, bf16[512,2048]{1,0:T(8,128)(2,1)} %get-tuple-element.8.wp_ref), custom_call_target="tpu_custom_call" | custom-call | tf_op jit(solution)/shard_map/project/pallas_call | solution.py:319
  71.0 1.7 %copy.7 = bf16[256,512]{1,0:T(8,128)(2,1)} copy(bf16[256,512]{1,0:T(8,128)(2,1)} %project.1) | data formatting | bytes 524288

commit v2 on v1

--- a/solution.py
+++ b/solution.py
@@ -9,7 +9,7 @@
 from jax.sharding import PartitionSpec as P
 
 R = 64
-T = 1024
+T = 512
 H = 16
 D = 128
 C = (D ** -0.5) * math.log2(math.e)
@@ -70,50 +70,43 @@
     )(q, w)
 
 
-def attn_kernel(U, NBUF, len_ref, q_own, q_recv, k_ref, v_ref, o_ref,
-                qv, q32, qt, kv, sbuf, o32, qsem, sem):
+def attn_kernel(U, NG, len_ref, q_own, q_recv, k_ref, v_ref, o_ref,
+                qv, q32, qt, kv, sbuf, pbuf, mbuf, lbuf, o32, l32, tbl, qsem, sem):
     me = lax.axis_index('dup')
     base = me * R
-
-    def fetch(idx, row, tile, slot, n, start):
-        length = len_ref[base + row]
-        rem = length - tile * T
-        pos = tile * T
-        def go(off, size):
-            if start:
-                for j, src in enumerate((k_ref, v_ref)):
-                    pltpu.make_async_copy(
-                        src.at[base + row, 0, pl.ds(pos + off, size), :],
-                        kv.at[slot, j, pl.ds(off, size), :], sem.at[slot]).start()
-            else:
-                part = kv.at[slot, :, pl.ds(off, size), :]
-                pltpu.make_async_copy(part, part, sem.at[slot]).wait()
-        full = jnp.logical_or(rem > 3 * T // 4, idx < NBUF)
-        valid = idx < n
-        @pl.when(jnp.logical_and(valid, full))
-        def _():
-            go(0, T)
-        @pl.when(jnp.logical_and(valid, jnp.logical_not(full)))
-        def _():
-            lax.fori_loop(0, (rem + T // 4 - 1) // (T // 4), lambda i, c: (go(i * (T // 4), T // 4), c)[1], 0)
-
-    def advance(row, tile):
-        length = len_ref[base + jnp.minimum(row, R - 1)]
-        done = (tile + 1) * T >= length
-        return jnp.where(done, jnp.minimum(row + 1, R - 1), row), jnp.where(done, 0, tile + 1)
+    HT = T // 2
+
+    def fetch_group(b, st):
+        row, tile = st
+        for u in range(U):
+            live = row < R
+            r = jnp.minimum(row, R - 1)
+            length = len_ref[base + r]
+            for j, src in enumerate((k_ref, v_ref)):
+                pltpu.make_async_copy(src.at[base + r, 0, pl.ds(pl.multiple_of(tile * T, T), T), :],
+                                      kv.at[b, u, j], sem.at[b]).start()
+            tbl[0, b * U + u] = row
+            tbl[1, b * U + u] = jnp.where(live, length - tile * T, 0)
+            tbl[2, b * U + u] = tile
+            done = jnp.logical_or((tile + 1) * T >= length, jnp.logical_not(live))
+            row, tile = jnp.where(done, jnp.minimum(row + 1, R), row), jnp.where(done, 0, tile + 1)
+        return row, tile
+
+    def wait_group(b):
+        pltpu.make_async_copy(kv.at[b], kv.at[b], sem.at[b]).wait()
 
     n = lax.fori_loop(0, R, lambda i, s: s + (len_ref[base + i] + T - 1) // T, jnp.int32(0))
+    ng = (n + U - 1) // U
 
     qcp = [pltpu.make_async_copy(q_recv.at[lax.rem(me + k, 4)], qv.at[lax.rem(me + k, 4)], qsem.at[k]) for k in range(1, 4)]
     qcp.append(pltpu.make_async_copy(q_own.at[pl.ds(base, R)], qv.at[me], qsem.at[0]))
     for c in qcp:
         c.start()
 
-    def prime(i, st):
-        row, tile = st
-        fetch(i, row, tile, i, n, True)
-        return advance(row, tile)
-    prow, ptile = lax.fori_loop(0, NBUF, prime, (jnp.int32(0), jnp.int32(0)))
+    z = jnp.int32(0)
+    def prime(b, st):
+        return fetch_group(b, st)
+    pst = lax.fori_loop(0, jnp.minimum(NG, ng), prime, (z, z))
 
     for c in qcp:
         c.wait()
@@ -127,93 +120,92 @@
         return 0
     lax.fori_loop(0, R, prep, 0, unroll=4)
 
-    HT = T // 2
     pos_i = (lax.broadcasted_iota(jnp.int32, (2 * H, HT), 0) // H) * HT + lax.broadcasted_iota(jnp.int32, (2 * H, HT), 1)
 
-    def scores(slot, row):
-        kab = jnp.concatenate([kv[slot, 0, 0:HT, :], kv[slot, 0, HT:T, :]], axis=1)
+    def scores(b, u, row):
+        kab = jnp.concatenate([kv[b, u, 0, 0:HT, :], kv[b, u, 0, HT:T, :]], axis=1)
         return lax.dot_general(qt[row], kab, (((1,), (1,)), ((), ())), preferred_element_type=jnp.float32)
 
-    def rest(jobs, ss):
-        ss = [jnp.where(pos_i < rem, s, NEG) for s, (_, _, rem) in zip(ss, jobs)]
-        ms = [jnp.max(jnp.maximum(s[0:H], s[H:]), axis=1, keepdims=True) for s in ss]
-        ps = [jnp.exp2((s - jnp.concatenate([m, m], 0)) * C) for s, m in zip(ss, ms)]
-        ls = [jnp.sum(p[0:H] + p[H:], axis=1, keepdims=True) for p in ps]
-        pbs = [p.astype(jnp.bfloat16) for p in ps]
+    wait_group(0)
+    for u in range(U):
+        sbuf[0, u] = scores(0, u, tbl[0, u])
+    pbuf[1] = jnp.zeros(pbuf.shape[1:], pbuf.dtype)
+    mbuf[1] = jnp.zeros(mbuf.shape[1:], mbuf.dtype)
+    lbuf[1] = jnp.zeros(lbuf.shape[1:], lbuf.dtype)
+
+    def stage(g, cur, carry):
+        pst, m0, l0, a0 = carry
+        oth = 1 - cur
+        bp = lax.rem(jnp.maximum(g - 1, 0), NG)
+        b = lax.rem(g, NG)
+        nb = lax.rem(g + 1, NG)
+
+        @pl.when(g + 1 < ng)
+        def _():
+            wait_group(nb)
         accs = []
-        for pb, (slot, _, _) in zip(pbs, jobs):
-            vab = jnp.concatenate([kv[slot, 1, 0:HT, :], kv[slot, 1, HT:T, :]], axis=1)
-            o2 = jnp.dot(pb, vab, preferred_element_type=jnp.float32)
+        for u in range(U):
+            vab = jnp.concatenate([kv[bp, u, 1, 0:HT, :], kv[bp, u, 1, HT:T, :]], axis=1)
+            o2 = jnp.dot(pbuf[oth, u], vab, preferred_element_type=jnp.float32)
             accs.append(o2[0:H, 0:D] + o2[H:, D:])
-        return list(zip(ms, ls, accs))
-
-    NG = NBUF // U
-    def group(g, crow, ctile):
-        infos = []
-        for u in range(U):
-            infos.append((g * U + u, lax.rem(g, NG) * U + u, crow, ctile))
-            crow, ctile = advance(crow, ctile)
-        return infos, crow, ctile
-
-    def wait_group(infos):
-        for idx, slot, row, tile in infos:
-            fetch(idx, row, tile, slot, n, False)
-
-    def body(g, carry):
-        prow, ptile, crow, ctile, m0, l0, a0 = carry
-        infos, nrow, ntile = group(g, crow, ctile)
-        nxt, _, _ = group(g + 1, nrow, ntile)
-        wait_group(nxt)
-        jobs = [(slot, row, jnp.where(idx < n, len_ref[base + row] - tile * T, 0)) for idx, slot, row, tile in infos]
-        cur, oth = lax.rem(g, 2), lax.rem(g + 1, 2)
-        ss = [sbuf[cur, u] for u in range(U)]
-        nss = [scores(slot, row) for _, slot, row, _ in nxt]
-        outs = rest(jobs, ss)
-        for (idx, slot, row, tile), (m, l, acc) in zip(infos, outs):
-            mp = jnp.where(tile == 0, NEG, m0)
-            mn = jnp.maximum(mp, m)
+        for u in range(U):
+            sbuf[oth, u] = scores(nb, u, jnp.where(g + 1 < ng, tbl[0, nb * U + u], 0))
+        for u in range(U):
+            s = jnp.where(pos_i < jnp.where(g < ng, tbl[1, b * U + u], 0), sbuf[cur, u], NEG)
+            m = jnp.max(jnp.maximum(s[0:H], s[H:]), axis=1, keepdims=True)
+            p = jnp.exp2((s - jnp.concatenate([m, m], 0)) * C)
+            pbuf[cur, u] = p.astype(jnp.bfloat16)
+            mbuf[cur, u] = jnp.broadcast_to(m, (H, D))
+            lbuf[cur, u] = jnp.broadcast_to(jnp.sum(p[0:H] + p[H:], axis=1, keepdims=True), (H, D))
+        for u in range(U):
+            mi = mbuf[oth, u]
+            mp = jnp.where(tbl[2, bp * U + u] == 0, NEG, m0)
+            mn = jnp.maximum(mp, mi)
             a = jnp.exp2((mp - mn) * C)
-            b = jnp.exp2((m - mn) * C)
+            c = jnp.exp2((mi - mn) * C)
             m0 = mn
-            l0 = l0 * a + l * b
-            a0 = a0 * a + acc * b
-            orow = jnp.where(idx < n, row, R)
-            o32[orow] = a0 / l0
-        for u in range(U):
-            sbuf[oth, u] = nss[u]
-        for idx, slot, row, tile in infos:
-            fetch(idx + NBUF, prow, ptile, slot, n, True)
-            prow, ptile = advance(prow, ptile)
-        return prow, ptile, nrow, ntile, m0, l0, a0
-
-    first, _, _ = group(jnp.int32(0), jnp.int32(0), jnp.int32(0))
-    wait_group(first)
-    for u, (_, slot, row, _) in enumerate(first):
-        sbuf[0, u] = scores(slot, row)
-
-    z = jnp.int32(0)
-    init = (prow, ptile, z, z, jnp.full((H, 1), NEG, jnp.float32), jnp.ones((H, 1), jnp.float32), jnp.zeros((H, D), jnp.float32))
-    lax.fori_loop(0, (n + U - 1) // U, body, init)
+            l0 = l0 * a + lbuf[oth, u] * c
+            a0 = a0 * a + accs[u] * c
+            orow = pl.multiple_of(jnp.where(g - 1 < ng, tbl[0, bp * U + u], R) * H, H)
+            o32[pl.ds(orow, H), :] = a0
+            l32[pl.ds(orow, H), :] = l0
+
+        def refill(st):
+            return fetch_group(bp, st)
+        pst = lax.cond(jnp.logical_and(g >= 1, g - 1 + NG < ng), refill, lambda st: st, pst)
+        return pst, m0, l0, a0
+
+    def body(h, carry):
+        return stage(2 * h + 1, 1, stage(2 * h, 0, carry))
+
+    init = (pst, jnp.full((H, D), NEG, jnp.float32), jnp.ones((H, D), jnp.float32), jnp.zeros((H, D), jnp.float32))
+    lax.fori_loop(0, (ng + 2) // 2, body, init)
     for h in range(H):
-        o_ref[h] = o32[0:R, h, :].astype(jnp.bfloat16)
-
-
-def attention(q_own, q_recv, k, v, lens, U=4, NBUF=20):
+        o_ref[h] = (o32[pl.ds(h, R, stride=H), :] / l32[pl.ds(h, R, stride=H), :]).astype(jnp.bfloat16)
+
+
+def attention(q_own, q_recv, k, v, lens, U=8, NBUF=7):
     any_ = pl.BlockSpec(memory_space=pl.ANY)
+    NG = NBUF
     return pl.pallas_call(
-        functools.partial(attn_kernel, U, NBUF),
+        functools.partial(attn_kernel, U, NG),
         out_shape=jax.ShapeDtypeStruct((H, R, D), jnp.bfloat16),
         in_specs=[pl.BlockSpec(memory_space=pltpu.SMEM), any_, any_, any_, any_],
         out_specs=pl.BlockSpec(memory_space=pltpu.VMEM),
         scratch_shapes=[
             pltpu.VMEM((4, R, 4, D), jnp.bfloat16),
             pltpu.VMEM((R, H, D), jnp.float32),
-            pltpu.VMEM((R, 2 * H, 2 * D), jnp.bfloat16),
-            pltpu.VMEM((NBUF, 2, T, D), jnp.bfloat16),
+            pltpu.VMEM((R + 1, 2 * H, 2 * D), jnp.bfloat16),
+            pltpu.VMEM((NG, U, 2, T, D), jnp.bfloat16),
             pltpu.VMEM((2, U, 2 * H, T // 2), jnp.float32),
-            pltpu.VMEM((R + 1, H, D), jnp.float32),
+            pltpu.VMEM((2, U, 2 * H, T // 2), jnp.bfloat16),
+            pltpu.VMEM((2, U, H, D), jnp.float32),
+            pltpu.VMEM((2, U, H, D), jnp.float32),
+            pltpu.VMEM(((R + 1) * H, D), jnp.float32),
+            pltpu.VMEM(((R + 1) * H, D), jnp.float32),
+            pltpu.SMEM((3, NG * U), jnp.int32),
             pltpu.SemaphoreType.DMA((4,)),
-            pltpu.SemaphoreType.DMA((NBUF,)),
+            pltpu.SemaphoreType.DMA((NG,)),
         ],
         compiler_params=pltpu.CompilerParams(vmem_limit_bytes=56 * 2**20),
         name='attn',

time: 72.6 us -> 63.8 us (0.88)
  Pallas kernels: 71 us -> 62.2 us
    pallas_call x1, Pallas kernels: 38.7 us -> 29.8 us  [attention(): pl.pallas_call(functools.partial(attn_kernel, U, NG), out_shape=jax.Shape...]
where the time goes in v2:
time: 63.8 us; the launch traced here: 63.9 us
  Pallas kernels  62.2 us (97%)
  local copies, waits for them, and re-layouts  1.67 us (3%)
    pallas_call x1, Pallas kernels, attention(): pl.pallas_call(functools.partial(attn_kernel, U, NG), out_shape=jax.Shape...  29.8 us
    pallas_call x1, Pallas kernels, project(): pl.pallas_call(proj_kernel, out_shape=jax.ShapeDtypeStruct((256, 512), jn...  24.9 us
    pallas_call x1, Pallas kernels, spread(): pl.pallas_call(spread_kernel, out_shape=(jax.ShapeDtypeStruct((4, R, 4, D...  7.46 us
    unnamed x1, local copies, waits for them, and re-layouts  1.67 us

profile of v2, /device:TPU:0, one launch (start us, length us, event | category | flops | bytes accessed | tf_op | source)
XLA Modules:
  0.0 63.9 jit_solution(5311253894315149069)
XLA Ops:
  0.0 7.5 %spread.1 = (bf16[4,64,4,128]{3,2,1,0:T(4,128)(2,1)}, bf16[512,2048]{1,0:T(8,128)(2,1)}) custom-call(bf16[256,4,128]{2,1,0:T(4,128)(2,1)} %q_own.1, bf16[512,4096]{1,0:T(8,128)(2,1)} %w_ref.3), custom_call_target="tpu_custom_call" | custom-call | tf_op jit(solution)/shard_map/spread/pallas_call | solution.py:63
  7.5 29.8 %attn.1.o_ref = bf16[16,64,128]{2,1,0:T(8,128)(2,1)} custom-call(s32[256]{0:T(256)} %len_ref.1, bf16[256,4,128]{2,1,0:T(4,128)(2,1)} %q_own.1, bf16[4,64,4,128]{3,2,1,0:T(4,128)(2,1)} %get-tuple-element.7.q_recv, bf16[256,1,4096,128]{3,2,1,0:T(8,128)(2,1)} %k_ref.1, bf16[256,1,4096,128]{3,2,1,0:T(8,128)(2,1)} %v_ref.1), custom_call_target="tpu_custom_call" | custom-call | tf_op jit(solution)/shard_map/attn/pallas_call | solution.py:190
  37.3 24.9 %project.1 = bf16[256,512]{1,0:T(8,128)(2,1)} custom-call(bf16[16,64,128]{2,1,0:T(8,128)(2,1)} %attn.1.o_ref, bf16[512,4096]{1,0:T(8,128)(2,1)} %w_ref.3, bf16[512,2048]{1,0:T(8,128)(2,1)} %get-tuple-element.8.wp_ref), custom_call_target="tpu_custom_call" | custom-call | tf_op jit(solution)/shard_map/project/pallas_call | solution.py:311
  62.2 1.7 %copy.7 = bf16[256,512]{1,0:T(8,128)(2,1)} copy(bf16[256,512]{1,0:T(8,128)(2,1)} %project.1) | data formatting | bytes 524288

commit v3 on v0

v3 whole, which is shorter than its diff:
```python
import functools
import math

import jax
import jax.numpy as jnp
from jax import lax
from jax.experimental import pallas as pl
from jax.experimental.pallas import tpu as pltpu
from jax.sharding import PartitionSpec as P

R = 64
R1 = 32
R2 = R - R1
K2 = 4
T = 512
HT = T // 2
U = 8
NG = 7
NG2 = 6
G2 = R2 * K2 // U
H = 16
D = 128
C = (D ** -0.5) * math.log2(math.e)
NEG = -3.0e38
MESH = pl.DeviceIdType.MESH
F32 = jnp.float32
BF16 = jnp.bfloat16


def _rcopy(src, dst, ssem, rsem, dev):
    return pltpu.make_async_remote_copy(src_ref=src, dst_ref=dst, send_sem=ssem, recv_sem=rsem,
                                        device_id=dev, device_id_type=MESH)


def _enter(peers):
    barrier = pltpu.get_barrier_semaphore()
    for p in peers:
        pl.semaphore_signal(barrier, inc=1, device_id=p, device_id_type=MESH)
    pl.semaphore_wait(barrier, len(peers))


def spread_kernel(q_ref, qr_ref, ssem, rsem):
    me = lax.axis_index('dup')
    _enter([{'dup': lax.rem(me + k, 4)} for k in (1, 2, 3)])
    cps = []
    for k in (2, 1, 3):
        to = lax.rem(me + k, 4)
        cps.append(_rcopy(q_ref.at[pl.ds(to * R, R)], qr_ref.at[me], ssem.at[k - 1], rsem.at[k - 1], {'dup': to}))
    for c in cps:
        c.start()
    for c in cps:
        c.wait()


def spread(q):
    any_ = pl.BlockSpec(memory_space=pl.ANY)
    dma = pltpu.SemaphoreType.DMA
    return pl.pallas_call(
        spread_kernel,
        out_shape=jax.ShapeDtypeStruct((4, R, 4, D), BF16),
        in_specs=[any_], out_specs=any_,
        scratch_shapes=[dma((3,)), dma((3,))],
        compiler_params=pltpu.CompilerParams(collective_id=0, has_side_effects=True),
        name='spread',
    )(q)


def _side_by_side(ref):
    return jnp.concatenate([ref[0:HT, :], ref[HT:T, :]], axis=1)


def _scores(q2, k):
    return lax.dot_general(q2, _side_by_side(k), (((1,), (1,)), ((), ())), preferred_element_type=F32)


def _weighted(p, v):
    o2 = jnp.dot(p, _side_by_side(v), preferred_element_type=F32)
    return o2[0:H, 0:D] + o2[H:, D:]


def _positions():
    half = lax.broadcasted_iota(jnp.int32, (2 * H, HT), 0) // H
    return half * HT + lax.broadcasted_iota(jnp.int32, (2 * H, HT), 1)


def _softmax(s, pos, rem, pbuf, mbuf, lbuf):
    s = jnp.where(pos < rem, s, NEG)
    m = jnp.max(jnp.maximum(s[0:H], s[H:]), axis=1, keepdims=True)
    p = jnp.exp2((s - jnp.concatenate([m, m], 0)) * C)
    pbuf[...] = p.astype(BF16)
    mbuf[...] = jnp.broadcast_to(m, (H, D))
    lbuf[...] = jnp.broadcast_to(jnp.sum(p[0:H] + p[H:], axis=1, keepdims=True), (H, D))


def _merge(state, m, l, acc):
    m0, l0, a0 = state
    mn = jnp.maximum(m0, m)
    a = jnp.exp2((m0 - mn) * C)
    c = jnp.exp2((m - mn) * C)
    return mn, l0 * a + l * c, a0 * a + acc * c


def attn_kernel(len_ref, q_own, q_recv, k_ref, v_ref, o_ref, st_ref, q2_ref,
                qv, q32, qt, kv, sbuf, pbuf, mbuf, lbuf, o32, l32, m32, rows, tbl, qsem, sem, osem):
    base = lax.axis_index('dup') * R
    me = lax.axis_index('dup')
    qcp = [pltpu.make_async_copy(q_recv.at[lax.rem(me + k, 4)], qv.at[lax.rem(me + k, 4)], qsem.at[k]) for k in range(1, 4)]
    qcp.append(pltpu.make_async_copy(q_own.at[pl.ds(base, R)], qv.at[me], qsem.at[0]))
    for c in qcp:
        c.start()

    def first_tile(row):
        return jnp.where(row < R1, 0, K2)

    def count(i, c):
        cnt, n = c
        items = jnp.maximum((len_ref[base + i] + T - 1) // T - first_tile(i), 0)
        rows[cnt] = i
        return cnt + jnp.where(items > 0, 1, 0), n + items

    cnt, n = lax.fori_loop(0, R, count, (jnp.int32(0), jnp.int32(0)), unroll=4)
    rows[cnt] = R
    ng = (n + U - 1) // U

    def fetch_group(b, st):
        k, tile = st
        for u in range(U):
            row = rows[k]
            live = row < R
            r = jnp.minimum(row, R - 1)
            length = len_ref[base + r]
            t = jnp.where(live, tile, 0)
            for j, src in enumerate((k_ref, v_ref)):
                pltpu.make_async_copy(src.at[base + r, 0, pl.ds(pl.multiple_of(t * T, T), T), :],
                                      kv.at[b, u, j], sem.at[b]).start()
            tbl[0, b * U + u] = row
            tbl[1, b * U + u] = jnp.where(live, length - t * T, 0)
            tbl[2, b * U + u] = jnp.where(t == first_tile(row), 1, 0)
            done = jnp.logical_and((tile + 1) * T >= length, live)
            k = jnp.where(done, k + 1, k)
            tile = jnp.where(done, first_tile(rows[k]), tile + 1)
        return k, tile

    def wait_group(b):
        pltpu.make_async_copy(kv.at[b], kv.at[b], sem.at[b]).wait()

    z = jnp.int32(0)
    pst = lax.fori_loop(0, jnp.minimum(NG, ng), fetch_group, (z, z))

    m32[...] = jnp.full(m32.shape, NEG, F32)
    l32[...] = jnp.zeros(l32.shape, F32)
    o32[...] = jnp.zeros(o32.shape, F32)
    pbuf[1] = jnp.zeros(pbuf.shape[1:], BF16)
    mbuf[1] = jnp.zeros(mbuf.shape[1:], F32)
    lbuf[1] = jnp.zeros(lbuf.shape[1:], F32)
    for c in qcp:
        c.wait()
    for s in range(4):
        q32[:, 4 * s:4 * s + 4, :] = qv[s].astype(F32)

    def prep(r, _):
        q16 = q32[r].astype(BF16)
        z16 = jnp.zeros_like(q16)
        qt[r] = jnp.concatenate([jnp.concatenate([q16, z16], 1), jnp.concatenate([z16, q16], 1)], 0)
        return 0
    lax.fori_loop(0, R, prep, 0, unroll=4)
    q2cp = pltpu.make_async_copy(qt.at[pl.ds(R1, R2)], q2_ref, osem.at[0])
    q2cp.start()

    pos = _positions()
    wait_group(0)
    for u in range(U):
        sbuf[0, u] = _scores(qt[tbl[0, u]], kv.at[0, u, 0])

    def stage(g, cur, carry):
        pst, state = carry
        oth = 1 - cur
        bp = lax.rem(jnp.maximum(g - 1, 0), NG)
        b = lax.rem(g, NG)
        nb = lax.rem(g + 1, NG)

        @pl.when(g + 1 < ng)
        def _():
            wait_group(nb)
        accs = [_weighted(pbuf[oth, u], kv.at[bp, u, 1]) for u in range(U)]
        for u in range(U):
            sbuf[oth, u] = _scores(qt[jnp.where(g + 1 < ng, tbl[0, nb * U + u], 0)], kv.at[nb, u, 0])
        for u in range(U):
            rem = jnp.where(g < ng, tbl[1, b * U + u], 0)
            _softmax(sbuf[cur, u], pos, rem, pbuf.at[cur, u], mbuf.at[cur, u], lbuf.at[cur, u])
        for u in range(U):
            m0, l0, a0 = state
            m0 = jnp.where(tbl[2, bp * U + u] == 1, NEG, m0)
            state = _merge((m0, l0, a0), mbuf[oth, u], lbuf[oth, u], accs[u])
            orow = pl.multiple_of(jnp.where(g - 1 < ng, tbl[0, bp * U + u], R) * H, H)
            for dst, val in zip((m32, l32, o32), state):
                dst[pl.ds(orow, H), :] = val
        pst = lax.cond(jnp.logical_and(g >= 1, g - 1 + NG < ng), lambda st: fetch_group(bp, st), lambda st: st, pst)
        return pst, state

    def body(h, carry):
        return stage(2 * h + 1, 1, stage(2 * h, 0, carry))

    state = (jnp.full((H, D), NEG, F32), jnp.ones((H, D), F32), jnp.zeros((H, D), F32))
    lax.fori_loop(0, (ng + 2) // 2, body, (pst, state))
    outs = [pltpu.make_async_copy(src.at[pl.ds(R1 * H, R2 * H)], st_ref.at[i], osem.at[i + 1])
            for i, src in enumerate((m32, l32, o32))]
    for c in outs:
        c.start()
    for h in range(H):
        o_ref[h] = (o32[pl.ds(h, R1, stride=H), :] / l32[pl.ds(h, R1, stride=H), :]).astype(BF16)
    for c in outs:
        c.wait()
    q2cp.wait()


def attention(q_own, q_recv, k, v, lens):
    any_ = pl.BlockSpec(memory_space=pl.ANY)
    dma = pltpu.SemaphoreType.DMA
    return pl.pallas_call(
        attn_kernel,
        out_shape=(jax.ShapeDtypeStruct((H, R1, D), BF16), jax.ShapeDtypeStruct((3, R2 * H, D), F32),
                   jax.ShapeDtypeStruct((R2, 2 * H, 2 * D), BF16)),
        in_specs=[pl.BlockSpec(memory_space=pltpu.SMEM), any_, any_, any_, any_],
        out_specs=(pl.BlockSpec(memory_space=pltpu.VMEM), any_, any_),
        scratch_shapes=[
            pltpu.VMEM((4, R, 4, D), BF16), pltpu.VMEM((R, H, D), F32), pltpu.VMEM((R + 1, 2 * H, 2 * D), BF16),
            pltpu.VMEM((NG, U, 2, T, D), BF16),
            pltpu.VMEM((2, U, 2 * H, HT), F32), pltpu.VMEM((2, U, 2 * H, HT), BF16),
            pltpu.VMEM((2, U, H, D), F32), pltpu.VMEM((2, U, H, D), F32),
            pltpu.VMEM(((R + 1) * H, D), F32), pltpu.VMEM(((R + 1) * H, D), F32), pltpu.VMEM(((R + 1) * H, D), F32),
            pltpu.SMEM((R + 1,), jnp.int32), pltpu.SMEM((3, NG * U), jnp.int32),
            dma((4,)), dma((NG,)), dma((4,)),
        ],
        compiler_params=pltpu.CompilerParams(vmem_limit_bytes=56 * 2**20),
        name='attn',
    )(lens, q_own, q_recv, k, v)


def tail_kernel(len_ref, o1_ref, st_ref, q2_ref, k_ref, v_ref, w_ref, y_ref,
                qt, st, kv, sbuf, pbuf, mbuf, lbuf, o2v, oc, wv, part, r1a, r1b, r2a, r2b,
                sem, lsem, wsem, wss, wsr, oss, osr, s1s, s1a, s1b, s2s, s2a, s2b):
    me = lax.axis_index('dup')
    kvi = lax.axis_index('kv')
    core = lax.rem(me, 2)
    x = me // 2
    ox, okv = 1 - x, 1 - kvi
    mate = me + 1 - 2 * core
    far = lax.rem(me + 2, 4)
    to_mate, to_x, to_y = {'dup': mate}, {'dup': far}, {'kv': okv}
    base = me * R + R1
    RR = R1

    def fetch_group(g):
        b = lax.rem(g, NG2)
        for u in range(U):
            i = g * U + u
            for j, src in enumerate((k_ref, v_ref)):
                pltpu.make_async_copy(src.at[base + i // K2, 0, pl.ds(pl.multiple_of(lax.rem(i, K2) * T, T), T), :],
                                      kv.at[b, u, j], sem.at[b]).start()

    def wait_group(g):
        b = lax.rem(g, NG2)
        pltpu.make_async_copy(kv.at[b], kv.at[b], sem.at[b]).wait()

    for g in range(2):
        fetch_group(jnp.int32(g))
    loads = [pltpu.make_async_copy(q2_ref, qt, lsem.at[0]), pltpu.make_async_copy(st_ref, st, lsem.at[1])]
    own = pltpu.make_async_copy(o1_ref.at[pl.ds(x * 8, 8)], oc.at[0, me], lsem.at[2])
    for c in loads + [own]:
        c.start()
    _enter([to_mate, to_x, to_y])

    def exchange(p, src):
        o_x = _rcopy(src.at[pl.ds(ox * 8, 8)], oc.at[p, me], oss.at[p, 0], osr.at[p, 0], to_x)
        o_m = _rcopy(src.at[pl.ds(x * 8, 8)], oc.at[p, me], oss.at[p, 1], osr.at[p, 1], to_mate)
        o_x.start()
        o_m.start()
        return o_x, o_m

    o_x, o_m = exchange(0, o1_ref)
    order = (okv * 2 + ox, kvi * 2 + ox, okv * 2 + x, kvi * 2 + x)
    wcps = []
    for i, j in enumerate(order):
        here = pl.multiple_of((j * 2 + core) * 512, 512)
        there = pl.multiple_of((j * 2 + 1 - core) * 512, 512)
        mine = wv.at[j, pl.ds(pl.multiple_of(core * 512, 512), 512)]
        wcps.append(pltpu.make_async_copy(w_ref.at[:, pl.ds(here, 512)], mine, wsem.at[i]))
        wcps.append(_rcopy(w_ref.at[:, pl.ds(there, 512)], mine, wss.at[j], wsr.at[j], to_mate))
    for c in wcps:
        c.start()
    for g in range(2, NG2):
        fetch_group(jnp.int32(g))

    pos = _positions()
    sends = []

    def forward(p, o_x):
        o_x.wait()
        fwd = _rcopy(oc.at[p, far], oc.at[p, far], oss.at[p, 2], osr.at[p, 2], to_mate)
        fwd.start()
        return fwd

    def multiply(p, t):
        X = x if t == 0 else ox
        lhs = jnp.concatenate(
            [jnp.concatenate([oc[p, 2 * X, h], oc[p, 2 * X + 1, h]], axis=0) for h in range(8)], axis=1)
        for i, j in enumerate(order):
            out = jnp.dot(lhs, wv[j], preferred_element_type=F32)
            part[p, X, j, 0] = out[:, :256]
            part[p, X, j, 1] = out[:, 256:]
            if i in (0, 1):
                k = okv if i == 0 else kvi
                sends.append(_rcopy(part.at[p, X, j, 0], r1a.at[p, X, k], s1s.at[p, t, 2 * i], s1a.at[p, X, k], to_x))
                sends[-1].start()
            if i in (0, 2):
                xx = ox if i == 0 else x
                sends.append(_rcopy(part.at[p, X, j, 1], r1b.at[p, X, xx], s1s.at[p, t, i + 1], s1b.at[p, X, xx], to_y))
                sends[-1].start()

    def arrived(dst, rsem, dev):
        _rcopy(dst, dst, s1s.at[0, 0, 0], rsem, dev).wait_recv()

    jm = kvi * 2 + x

    def second(p):
        for t in range(2):
            Xa = ox if t == 0 else x
            Xb = x if t == 0 else ox
            ja = okv * 2 + x
            arrived(r1a.at[p, Xa, okv], s1a.at[p, Xa, okv], to_x)
            part[p, Xa, ja, 0] = part[p, Xa, ja, 0] + r1a[p, Xa, okv]
            sends.append(_rcopy(part.at[p, Xa, ja, 0], r2a.at[p, Xa], s2s.at[p, t, 0], s2a.at[p, Xa], to_y))
            sends[-1].start()
            jb = kvi * 2 + ox
            arrived(r1b.at[p, Xb, ox], s1b.at[p, Xb, ox], to_y)
            part[p, Xb, jb, 1] = part[p, Xb, jb, 1] + r1b[p, Xb, ox]
            sends.append(_rcopy(part.at[p, Xb, jb, 1], r2b.at[p, Xb], s2s.at[p, t, 1], s2b.at[p, Xb], to_x))
            sends[-1].start()
            arrived(r1a.at[p, Xa, kvi], s1a.at[p, Xa, kvi], to_x)
            part[p, Xa, jm, 0] = part[p, Xa, jm, 0] + r1a[p, Xa, kvi]
            arrived(r1b.at[p, Xb, x], s1b.at[p, Xb, x], to_y)
            part[p, Xb, jm, 1] = part[p, Xb, jm, 1] + r1b[p, Xb, x]

    def finish(p):
        for t in range(2):
            X = ox if t == 0 else x
            arrived(r2a.at[p, X], s2a.at[p, X], to_y)
            arrived(r2b.at[p, X], s2b.at[p, X], to_x)
            for half, r in ((0, r2a), (1, r2b)):
                val = (part[p, X, jm, half] + r[p, X]).astype(BF16)
                for c in range(2):
                    row = pl.multiple_of(X * 2 * R + c * R + p * RR, RR)
                    y_ref[pl.ds(row, RR), half * 256:half * 256 + 256] = val[c * RR:(c + 1) * RR]

    def scores(g, oth):
        b = lax.rem(g, NG2)
        for u in range(U):
            sbuf[oth, u] = _scores(qt[(g * U + u) // K2], kv.at[b, u, 0])

    def stage(g, cur, state, qk=True, sm=True, pv=True):
        oth = 1 - cur
        if qk:
            wait_group(g + 1)
        accs = None
        bp = lax.rem(g - 1 + NG2, NG2)
        if pv:
            accs = [_weighted(pbuf[oth, u], kv.at[bp, u, 1]) for u in range(U)]
        if qk:
            scores(g + 1, oth)
        if sm:
            for u in range(U):
                i = g * U + u
                rem = len_ref[base + i // K2] - lax.rem(i, K2) * T
                _softmax(sbuf[cur, u], pos, rem, pbuf.at[cur, u], mbuf.at[cur, u], lbuf.at[cur, u])
        if pv:
            for u in range(U):
                i = (g - 1) * U + u
                at = pl.ds(pl.multiple_of((i // K2) * H, H), H)
                if u % K2 == 0:
                    state = (st[0, at, :], st[1, at, :], st[2, at, :])
                state = _merge(state, mbuf[oth, u], lbuf[oth, u], accs[u])
                if u % K2 == K2 - 1:
                    st[1, at, :] = state[1]
                    st[2, at, :] = state[2]
        if qk and pv:
            @pl.when(g - 1 + NG2 < G2)
            def _():
                fetch_group(g - 1 + NG2)
        return state

    def pair(h, state):
        return stage(2 * h + 2, 0, stage(2 * h + 1, 1, state))

    for c in loads:
        c.wait()
    wait_group(jnp.int32(0))
    scores(jnp.int32(0), 0)
    state = (jnp.zeros((H, D), F32),) * 3
    stage(jnp.int32(0), 0, state, pv=False)
    last = (G2 - 2) // 2
    state = lax.fori_loop(0, last // 2 - 1, pair, state)
    fwd = forward(0, o_x)
    own.wait()
    o_m.wait()
    for c in wcps:
        c.wait()
    multiply(0, 0)
    state = lax.fori_loop(last // 2 - 1, last // 2, pair, state)
    fwd.wait()
    multiply(0, 1)
    state = lax.fori_loop(last // 2, last, pair, state)
    stage(jnp.int32(G2 - 1), 1, state, qk=False)
    stage(jnp.int32(G2), 0, state, qk=False, sm=False)
    for h in range(H):
        o2v[h] = (st[2, pl.ds(h, R2, stride=H), :] / st[1, pl.ds(h, R2, stride=H), :]).astype(BF16)
    o_x, o_m = exchange(1, o2v)
    oc[1, me] = o2v[pl.ds(x * 8, 8)]
    second(0)
    o_m.wait()
    multiply(1, 0)
    fwd = forward(1, o_x)
    finish(0)
    fwd.wait()
    multiply(1, 1)
    second(1)
    finish(1)
    for c in sends:
        c.wait_send()


def tail(lens, o1, st, q2, k, v, w):
    any_ = pl.BlockSpec(memory_space=pl.ANY)
    dma = pltpu.SemaphoreType.DMA
    M = 2 * R1
    return pl.pallas_call(
        tail_kernel,
        out_shape=jax.ShapeDtypeStruct((256, 512), BF16),
        in_specs=[pl.BlockSpec(memory_space=pltpu.SMEM)] + [any_] * 6, out_specs=pl.BlockSpec(memory_space=pltpu.VMEM),
        scratch_shapes=[
            pltpu.VMEM((R2, 2 * H, 2 * D), BF16), pltpu.VMEM((3, R2 * H, D), F32),
            pltpu.VMEM((NG2, U, 2, T, D), BF16),
            pltpu.VMEM((2, U, 2 * H, HT), F32), pltpu.VMEM((2, U, 2 * H, HT), BF16),
            pltpu.VMEM((2, U, H, D), F32), pltpu.VMEM((2, U, H, D), F32),
            pltpu.VMEM((H, R2, D), BF16),
            pltpu.VMEM((2, 4, 8, R1, D), BF16), pltpu.VMEM((4, 1024, 512), BF16),
            pltpu.VMEM((2, 2, 4, 2, M, 256), F32),
            pltpu.VMEM((2, 2, 2, M, 256), F32), pltpu.VMEM((2, 2, 2, M, 256), F32),
            pltpu.VMEM((2, 2, M, 256), F32), pltpu.VMEM((2, 2, M, 256), F32),
            dma((NG2,)), dma((3,)), dma((4,)), dma((4,)), dma((4,)), dma((2, 3)), dma((2, 3)),
            dma((2, 2, 4)), dma((2, 2, 2)), dma((2, 2, 2)),
            dma((2, 2, 2)), dma((2, 2)), dma((2, 2)),
        ],
        compiler_params=pltpu.CompilerParams(collective_id=1, has_side_effects=True, vmem_limit_bytes=48 * 2**20),
        name='tail',
    )(lens, o1, st, q2, k, v, w)


def solution(mesh):
    def per_device(q, k, v, lens, w):
        q_recv = spread(q)
        o1, st, q2 = attention(q, q_recv, k, v, lens)
        return tail(lens, o1, st, q2, k, v, w)

    return jax.shard_map(
        per_device,
        mesh=mesh,
        in_specs=(P('dp', ('kv', 'dup'), None), P('dp', 'kv', None, None), P('dp', 'kv', None, None), P('dp'), P(('kv', 'dup'), None)),
        out_specs=P('dp', ('kv', 'dup')),
        check_vma=False,
    )
```

time: 175 us -> 67.1 us (0.38)
  waiting for transfers between devices: 72.7 us -> 0 us
  matrix products: 65 us -> 0 us
  Pallas kernels: 0 us -> 62.8 us
  between operations: 13.5 us -> 0.07 us
  other arithmetic: 12.7 us -> 0 us
  starting transfers between devices: 6.82 us -> 0 us
    dot_general x3 -> x0, matrix products: 65 us -> none  [the longest x1 31.2 us: per_device(): jnp.einsum('bgd,bsd->bgs', q_group, k_span, preferred_element_type=jnp.fl...]
    pallas_call x0 -> x3, Pallas kernels: none -> 62.8 us  [the longest x1 34.2 us: tail(): pl.pallas_call(tail_kernel, out_shape=jax.ShapeDtypeStruct((256, 512), BF...]
    reduce_scatter x1 -> x0, waiting for transfers between devices: 42.6 us -> none  [per_device(): lax.psum_scatter(proj_part, ('kv', 'dup'), scatter_dimension=1, tiled=True)]
    all_gather x1 -> x0, waiting for transfers between devices: 16.3 us -> none  [per_device(): q_group = lax.all_gather(q_loc, 'dup', axis=1, tiled=True)]
    all_to_all x2 -> x0, waiting for transfers between devices: 13.8 us -> none  [the longest x1 13.8 us: per_device(): lax.all_to_all(partial, 'dup', split_axis=1, concat_axis=1, tiled=True)]
    reduce_sum x3 -> x0, other arithmetic: 10 us -> none  [the longest x1 8.31 us: per_device(): prob_sum = jnp.sum(weights, axis=-1)]
    all_to_all x2 -> x0, starting transfers between devices: 6.78 us -> none  [the longest x1 3.52 us: per_device(): lax.all_to_all(partial, 'dup', split_axis=1, concat_axis=1, tiled=True)]
    unnamed x1 -> x11, local copies, waits for them, and re-layouts: 1.69 us -> 3.79 us
  transfers between devices with their start and end apart: 4 -> 0, of which waited for: 3 -> 0; matrix products, arithmetic and copies ran while one was open for 18% -> 0% of each run, Pallas kernels for 0% -> 0%
where the time goes in v3:
time: 67.1 us; the launch traced here: 66.7 us
  Pallas kernels  62.8 us (94%)
  local copies, waits for them, and re-layouts  3.79 us (6%)
    pallas_call x1, Pallas kernels, tail(): pl.pallas_call(tail_kernel, out_shape=jax.ShapeDtypeStruct((256, 512), BF...  34.2 us
    pallas_call x1, Pallas kernels, attention(): pl.pallas_call(attn_kernel, out_shape=(jax.ShapeDtypeStruct((H, R1, D), B...  21.3 us
    pallas_call x1, Pallas kernels, spread(): pl.pallas_call(spread_kernel, out_shape=jax.ShapeDtypeStruct((4, R, 4, D)...  7.38 us
    unnamed x11, local copies, waits for them, and re-layouts  3.79 us

profile of v3, /device:TPU:0, one launch (start us, length us, event | category | flops | bytes accessed | tf_op | source)
XLA Modules:
  0.0 66.7 jit_solution(15213643171534624869)
XLA Ops:
  0.0 7.4 %spread.1.q_recv = bf16[4,64,4,128]{3,2,1,0:T(4,128)(2,1)} custom-call(bf16[256,4,128]{2,1,0:T(4,128)(2,1)} %q_own.1), custom_call_target="tpu_custom_call" | custom-call | tf_op jit(solution)/shard_map/spread/pallas_call | solution.py:58
  7.4 0.0 copy-start
  7.4 0.0 copy-start.4
  7.4 21.3 %attn.1 = (bf16[16,32,128]{2,1,0:T(8,128)(2,1)}, f32[3,512,128]{2,1,0:T(8,128)}, bf16[32,32,256]{2,1,0:T(8,128)(2,1)}) custom-call(s32[256]{0:T(256)} %len_ref.3, bf16[256,4,128]{2,1,0:T(4,128)(2,1)} %q_own.1, bf16[4,64,4,128]{3,2,1,0:T(4,128)(2,1)} %spread.1.q_recv, bf16[256,1,4096,128]{3,2,1,0:T(8,128)(2,1)} %k_ref.3, bf16[256,1,4096,128]{3,2,1,0:T(8,128)(2,1)} %v_ref.3), custom_call_target="tpu_custom_call" | custom-call | tf_op jit(solution)/shard_map/attn/pallas_call | solution.py:220
  28.7 0.0 copy-done
  28.7 0.0 copy-done.4
  28.7 0.0 copy-start.1
  28.7 1.1 %copy-done.1 = f32[3,512,128]{2,1,0:T(8,128)S(1)} copy-done((f32[3,512,128]{2,1,0:T(8,128)S(1)}, f32[3,512,128]{2,1,0:T(8,128)}, u32[]{:S(2)}) %copy-start.1) | copy-done | bytes 786456
  29.8 0.0 copy-start.2
  29.8 1.0 %copy-done.2 = bf16[32,32,256]{2,1,0:T(8,128)(2,1)S(1)} copy-done((bf16[32,32,256]{2,1,0:T(8,128)(2,1)S(1)}, bf16[32,32,256]{2,1,0:T(8,128)(2,1)}, u32[]{:S(2)}) %copy-start.2) | copy-done | bytes 524312
  30.9 0.0 copy-start.3
  30.9 0.9 %copy-done.3 = bf16[16,32,128]{2,1,0:T(8,128)(2,1)S(1)} copy-done((bf16[16,32,128]{2,1,0:T(8,128)(2,1)S(1)}, bf16[16,32,128]{2,1,0:T(8,128)(2,1)}, u32[]{:S(2)}) %copy-start.3) | copy-done | bytes 131096
  31.8 34.2 %tail.1 = bf16[256,512]{1,0:T(8,128)(2,1)S(1)} custom-call(s32[256]{0:T(256)S(1)} %copy-done.4, bf16[16,32,128]{2,1,0:T(8,128)(2,1)S(1)} %copy-done.3, f32[3,512,128]{2,1,0:T(8,128)S(1)} %copy-done.1, bf16[32,32,256]{2,1,0:T(8,128)(2,1)S(1)} %copy-done.2, bf16[256,1,4096,128]{3,2,1,0:T(8,128)(2,1)} %k_ref.3, bf16[256,1,4096,128]{3,2,1,0:T(8,128)(2,1)} %v_ref.3, ...), custom_call_target="tpu_custom_call" | custom-call | tf_op jit(solution)/shard_map/tail/pallas_call | solution.py:436
  66.0 0.7 %copy.7 = bf16[256,512]{1,0:T(8,128)(2,1)} copy(bf16[256,512]{1,0:T(8,128)(2,1)S(1)} %tail.1) | data formatting | bytes 524288
Async XLA Ops:
  7.4 21.3 %copy-start = (bf16[512,4096]{1,0:T(8,128)(2,1)S(1)}, bf16[512,4096]{1,0:T(8,128)(2,1)}, u32[]{:S(2)}) copy-start(bf16[512,4096]{1,0:T(8,128)(2,1)} %w_ref.1) | copy-start | bytes 12582916
  7.4 21.3 %copy-start.4 = (s32[256]{0:T(256)S(1)}, s32[256]{0:T(256)}, u32[]{:S(2)}) copy-start(s32[256]{0:T(256)} %len_ref.3) | copy-start | bytes 3076
  28.7 1.1 %copy-start.1 = (f32[3,512,128]{2,1,0:T(8,128)S(1)}, f32[3,512,128]{2,1,0:T(8,128)}, u32[]{:S(2)}) copy-start(f32[3,512,128]{2,1,0:T(8,128)} %get-tuple-element.9.st_ref) | copy-start | bytes 2359300
  29.8 1.0 %copy-start.2 = (bf16[32,32,256]{2,1,0:T(8,128)(2,1)S(1)}, bf16[32,32,256]{2,1,0:T(8,128)(2,1)}, u32[]{:S(2)}) copy-start(bf16[32,32,256]{2,1,0:T(8,128)(2,1)} %get-tuple-element.10.q2_ref) | copy-start | bytes 1572868
  30.9 0.9 %copy-start.3 = (bf16[16,32,128]{2,1,0:T(8,128)(2,1)S(1)}, bf16[16,32,128]{2,1,0:T(8,128)(2,1)}, u32[]{:S(2)}) copy-start(bf16[16,32,128]{2,1,0:T(8,128)(2,1)} %get-tuple-element.8.o1_ref) | copy-start | bytes 393220
